TPU v7x, 16 devices: a whole 2x2x2 slice. The times are simulated.
16 devices in a mesh: data: 4 (over z, y), sp: 4 (over x, core).
Axes of the slice: x: 2, y: 2, z: 2, core: 2. Of those that a mesh axis runs over, the one named last changes fastest.
Arguments:
- latent: bfloat16 [4, 128, 256, 384], P('data', 'sp'), parts along dimension 0
- ln_gain: bfloat16 [4, 384], replicated
- ln_bias: bfloat16 [4, 384], replicated
- w_qkv: bfloat16 [2, 384, 3, 6, 64], replicated
- w_out: bfloat16 [2, 6, 64, 384], replicated
- w_up: bfloat16 [2, 384, 1536], replicated
- w_down: bfloat16 [2, 1536, 384], replicated
Outputs:
- output: bfloat16 [4, 128, 256, 384], P('data', 'sp'), parts along dimension 0
There are 4 independent parts. A program takes and returns all parts, laid end to end along the dimension named above; an argument that names none is the same for every part.
All inputs are finite; a program needn't handle non-finite values.
Results may differ from a plain program's by a relative error of at most 0.0114142.
Values are sent between devices in bfloat16 or wider.
A program may use at most 1 GiB of HBM per device.

v0:
```python
import jax
import jax.numpy as jnp
from jax import lax
from jax.sharding import PartitionSpec as P, NamedSharding

LN_EPS = 1e-6
SPACE_FORMS = ('btqhk,btphk->bthqp', 'bthqp,btphk->btqhk')
TIME_FORMS = ('bqshk,bpshk->bshqp', 'bshqp,bpshk->bqshk')


def layer_norm(tokens, gain_vec, shift_vec):
    as_float = tokens.astype(jnp.float32)
    mean_val = jnp.mean(as_float, axis=-1, keepdims=True)
    centered = as_float - mean_val
    variance = jnp.mean(centered * centered, axis=-1, keepdims=True)
    normed = centered * lax.rsqrt(variance + LN_EPS) * gain_vec.astype(jnp.float32) + shift_vec.astype(jnp.float32)
    return normed.astype(jnp.bfloat16)


def project_qkv(tokens, gain_vec, shift_vec, w_qkv_blk):
    normed = layer_norm(tokens, gain_vec, shift_vec)
    return jnp.einsum('btsd,dchk->btschk', normed, w_qkv_blk, preferred_element_type=jnp.float32).astype(jnp.bfloat16)


def attend(qkv_all, ein_forms):
    score_scale = qkv_all.shape[-1] ** -0.5
    query_rows = qkv_all[:, :, :, 0]
    key_rows = qkv_all[:, :, :, 1]
    value_rows = qkv_all[:, :, :, 2]
    scores = jnp.einsum(ein_forms[0], query_rows, key_rows, preferred_element_type=jnp.float32) * score_scale
    attn_probs = jax.nn.softmax(scores, axis=-1).astype(jnp.bfloat16)
    return jnp.einsum(ein_forms[1], attn_probs, value_rows, preferred_element_type=jnp.float32).astype(jnp.bfloat16)


def finish_block(tokens, attended, gain_vec, shift_vec, w_out_blk, w_up_blk, w_down_blk):
    projected = jnp.einsum('btshk,hkd->btsd', attended, w_out_blk, preferred_element_type=jnp.float32)
    residual = (tokens.astype(jnp.float32) + projected).astype(jnp.bfloat16)
    normed = layer_norm(residual, gain_vec, shift_vec)
    hidden = jax.nn.gelu(jnp.einsum('btsd,df->btsf', normed, w_up_blk, preferred_element_type=jnp.float32), approximate=True).astype(jnp.bfloat16)
    result = residual.astype(jnp.float32) + jnp.einsum('btsf,fd->btsd', hidden, w_down_blk, preferred_element_type=jnp.float32)
    return result.astype(jnp.bfloat16)


def value_a9(tokens, layer_idx, ein_forms, ln_gain, ln_bias, w_qkv, w_out, w_up, w_down):
    qkv_all = project_qkv(tokens, ln_gain[2 * layer_idx], ln_bias[2 * layer_idx], w_qkv[layer_idx])
    attended = attend(qkv_all, ein_forms)
    return finish_block(tokens, attended, ln_gain[2 * layer_idx + 1], ln_bias[2 * layer_idx + 1], w_out[layer_idx], w_up[layer_idx], w_down[layer_idx])


def solution(mesh):
    act_spec = P('data', 'sp', None, None)

    def local_run(local_latent, ln_gain, ln_bias, w_qkv, w_out, w_up, w_down):
        mixed_act = value_a9(local_latent, 0, SPACE_FORMS, ln_gain, ln_bias, w_qkv, w_out, w_up, w_down)
        mixed_act = lax.all_to_all(mixed_act, 'sp', 2, 1, tiled=True)
        mixed_act = value_a9(mixed_act, 1, TIME_FORMS, ln_gain, ln_bias, w_qkv, w_out, w_up, w_down)
        return lax.all_to_all(mixed_act, 'sp', 1, 2, tiled=True)

    return jax.shard_map(local_run, mesh=mesh, in_specs=(act_spec, P(), P(), P(), P(), P(), P()), out_specs=act_spec, check_vma=False)
```

profile of v0, /device:TPU:0, one launch (start us, length us, event | category | flops | bytes accessed | tf_op | source)
XLA Modules:
  0.0 432.9 jit_solution(12826800091940063965)
XLA Ops:
  0.0 4.1 convert_reduce_fusion.2
  4.1 5.2 %fusion.44 = f32[32,256]{1,0:T(8,128)S(1)} fusion(bf16[1,32,256,384]{3,2,1,0:T(8,128)(2,1)} %param.7, f32[32,256]{1,0:T(8,128)S(1)} %broadcast_multiply_fusion.3), kind=kLoop, calls=%fused_computation.57 | loop fusion | flops 12574720 | bytes 6356992 | tf_op jit(solution)/shard_map/reduce_sum | solution.py:15
  9.3 0.0 copy-done.3
  9.3 0.0 copy-done.2
  9.3 0.6 convert_reduce_fusion.3
  9.9 0.0 copy-done.8
  10.0 16.1 %convert_bitcast_fusion.1 = bf16[1,32,256,3,6,64]{2,5,4,3,1,0:T(8,128)(2,1)} fusion(bf16[1,32,256,384]{3,2,1,0:T(8,128)(2,1)} %param.7, f32[384]{0:T(512)S(1)} %get-tuple-element.11, f32[384]{0:T(512)S(1)} %get-tuple-element.22, f32[32,256]{1,0:T(8,128)S(1)} %add_rsqrt_fusion.3, f32[32,256]{1,0:T(8,128)S(1)} %broadcast_multiply_fusion.3, ...), kind=kOutput, calls=%fused_computation.42 | convolution fusion | flops 7276068864 | bytes 26120192 | tf_op jit(solution)/shard_map/btsd,dchk->btschk/dot_general | solution.py:22
  26.0 25.2 %fusion.140 = (f32[32,6,256]{2,1,0:T(8,128)S(1)}, f32[32,6,256,256]{2,3,1,0:T(8,128)}) fusion(bf16[1,32,256,3,6,64]{2,5,4,3,1,0:T(8,128)(2,1)} %convert_bitcast_fusion.1), kind=kOutput, calls=%fused_computation.146 | convolution fusion | flops 1648361728 | bytes 63111168 | tf_op jit(solution)/shard_map/sub | solution.py:31
  51.2 0.0 copy-done.10
  51.2 25.6 %convert_reduce_fusion.1 = (f32[32,256]{1,0:T(8,128)S(1)}, bf16[1,32,256,384]{3,2,1,0:T(8,128)(2,1)}) fusion(bf16[2,6,64,384]{3,2,1,0:T(8,128)(2,1)S(1)} %copy-done.10, f32[32,6,256,256]{2,3,1,0:T(8,128)} %get-tuple-element.14, f32[32,6,256]{2,1,0:T(8,128)S(1)} %get-tuple-element.13, bf16[1,32,256,3,6,64]{2,5,4,3,1,0:T(8,128)(2,1)} %convert_bitcast_fusion.1, ...), kind=kOutput, calls=%fused_computation.37 | convolution fusion | flops 4070563840 | bytes 69795840 | tf_op jit(solution)/shard_map/btshk,hkd->btsd/dot_general | solution.py:36
  76.8 5.2 %fusion.40 = f32[32,256]{1,0:T(8,128)S(1)} fusion(bf16[1,32,256,384]{3,2,1,0:T(8,128)(2,1)} %get-tuple-element.16, f32[32,256]{1,0:T(8,128)S(1)} %broadcast_multiply_fusion.2), kind=kLoop, calls=%fused_computation.53 | loop fusion | flops 12574720 | bytes 6356992 | tf_op jit(solution)/shard_map/reduce_sum | solution.py:15
  82.0 0.6 add_rsqrt_fusion.2
  82.6 0.1 fusion.170
  82.8 44.4 %fusion.49 = bf16[1,32,256,384]{3,2,1,0:T(8,128)(2,1)} fusion(bf16[1,32,256,384]{3,2,1,0:T(8,128)(2,1)} %get-tuple-element.16, f32[384]{0:T(512)S(1)} %get-tuple-element.10, f32[384]{0:T(512)S(1)} %get-tuple-element.23, f32[32,256]{1,0:T(8,128)} %add_rsqrt_fusion.2, f32[32,256]{1,0:T(8,128)} %copy-done.1, bf16[2,384,1536]{2,1,0:T(8,128)(2,1)} %param.12, ...), kind=kOutput, calls=%fused_computation.62 | convolution fusion | flops 19468910592 | bytes 21302272 | tf_op jit(solution)/shard_map/btsf,fd->btsd/dot_general | solution.py:40
  127.2 9.2 %copy.14 = bf16[1,32,256,384]{3,1,0,2:T(8,128)(2,1)} copy(bf16[1,32,256,384]{3,2,1,0:T(8,128)(2,1)} %fusion.49) | data formatting | bytes 12582912 | tf_op jit(solution)/shard_map/convert_element_type | solution.py:41
  136.4 5.2 %all-to-all-start = ((bf16[1,32,256,384]{3,1,0,2:T(8,128)(2,1)}), bf16[1,32,256,384]{3,1,0,2:T(8,128)(2,1)}, u32[]{:S(2)}, u32[]{:S(2)}) async-start(bf16[1,32,256,384]{3,1,0,2:T(8,128)(2,1)} %copy.14), calls=%async_computation | async-start | bytes 12582912 | tf_op jit(solution)/shard_map/all_to_all | solution.py:55
  141.6 0.1 fusion.172
  141.8 71.2 %all-to-all-done = bf16[1,32,256,384]{3,1,0,2:T(8,128)(2,1)} async-done(((bf16[1,32,256,384]{3,1,0,2:T(8,128)(2,1)}), bf16[1,32,256,384]{3,1,0,2:T(8,128)(2,1)}, u32[]{:S(2)}, u32[]{:S(2)}) %all-to-all-start) | async-done | bytes 6291488 | tf_op jit(solution)/shard_map/all_to_all | solution.py:55
  212.9 4.0 bitcast_reduce_fusion
  216.9 9.2 %copy.15 = f32[1,32,4,64,384]{4,1,2,3,0:T(8,128)} copy(bf16[1,32,4,64,384]{4,1,3,2,0:T(8,128)(2,1)} %bitcast.54) | data formatting | bytes 18874368 | tf_op jit(solution)/shard_map/convert_element_type | solution.py:37
  226.2 5.5 %multiply_reduce_fusion.2 = f32[4,32,64]{1,0,2:T(4,128)S(1)} fusion(f32[4,32,64]{1,0,2:T(4,128)S(1)} %broadcast_multiply_fusion, bf16[1,32,4,64,384]{4,1,3,2,0:T(8,128)(2,1)} %bitcast.54), kind=kLoop, calls=%fused_computation.70 | loop fusion | flops 12574720 | bytes 6356992 | tf_op jit(solution)/shard_map/reduce_sum | solution.py:15
  231.7 0.1 add_rsqrt_fusion
  231.8 5.8 %add_convert_fusion = bf16[1,4,32,64,384]{4,2,1,3,0:T(8,128)(2,1)S(1)} fusion(f32[384]{0:T(512)S(1)} %copy-done.4, f32[384]{0:T(512)S(1)} %copy-done.5, f32[4,32,64]{1,0,2:T(4,128)S(1)} %add_rsqrt_fusion, f32[4,32,64]{1,0,2:T(4,128)S(1)} %broadcast_multiply_fusion, bf16[1,32,4,64,384]{4,1,3,2,0:T(8,128)(2,1)} %bitcast.54), kind=kLoop, calls=%fused_computation.69 | loop fusion | flops 18874368 | bytes 12651520 | tf_op jit(solution)/shard_map/convert_element_type | solution.py:17
  237.5 12.9 %convert_bitcast_fusion = bf16[1,128,64,3,6,64]{1,5,4,3,2,0:T(8,128)(2,1)} fusion(bf16[128,64,384,1,1]{2,0,4,3,1:T(8,128)(2,1)S(1)} %bitcast.189, bf16[2,384,3,6,64]{1,4,3,2,0:T(8,128)(2,1)S(1)} %copy-done.9), kind=kOutput, calls=%fused_computation.41 | convolution fusion | flops 7257194496 | bytes 26050560 | tf_op jit(solution)/shard_map/btsd,dchk->btschk/dot_general | solution.py:22
  250.4 12.9 %fusion.70 = f32[64,6,128,128]{2,3,1,0:T(8,128)} fusion(bf16[1,128,64,3,6,64]{1,5,4,3,2,0:T(8,128)(2,1)} %convert_bitcast_fusion), kind=kOutput, calls=%fused_computation.79 | convolution fusion | flops 805306368 | bytes 37748736 | tf_op jit(solution)/shard_map/bqshk,bpshk->bshqp/dot_general | solution.py:30
  263.4 27.2 %fusion.141 = (f32[64,6,128]{2,1,0:T(8,128)S(1)}, f32[64,6,128,128]{2,3,1,0:T(8,128)}) fusion(f32[64,6,128,128]{2,3,1,0:T(8,128)} %fusion.70), kind=kOutput, calls=%fused_computation.147 | output fusion | flops 25165952 | bytes 50528256 | tf_op jit(solution)/shard_map/sub | solution.py:31
  290.6 18.9 %convert_reduce_fusion = (f32[128,64]{0,1:T(8,128)S(1)}, bf16[128,64,384]{2,0,1:T(8,128)(2,1)}) fusion(f32[128,64,384]{2,0,1:T(8,128)} %bitcast.188, bf16[2,6,64,384]{3,2,1,0:T(8,128)(2,1)S(1)} %copy-done.11, f32[64,6,128,128]{2,3,1,0:T(8,128)} %get-tuple-element.18, f32[64,6,128]{2,1,0:T(8,128)S(1)} %get-tuple-element.17, ...), kind=kOutput, calls=%fused_computation.34 | convolution fusion | flops 3249528832 | bytes 50921472 | tf_op jit(solution)/shard_map/btshk,hkd->btsd/dot_general | solution.py:36
  309.5 5.3 %fusion.36 = f32[128,64]{0,1:T(8,128)S(1)} fusion(bf16[128,64,384]{2,0,1:T(8,128)(2,1)} %get-tuple-element.20, f32[128,64]{0,1:T(8,128)S(1)} %broadcast_multiply_fusion.1), kind=kLoop, calls=%fused_computation.49 | loop fusion | flops 12574720 | bytes 6356992 | tf_op jit(solution)/shard_map/reduce_sum | solution.py:15
  314.9 34.2 %fusion.58 = bf16[1,128,64,384]{3,1,2,0:T(8,128)(2,1)} fusion(bf16[128,64,384]{2,0,1:T(8,128)(2,1)} %get-tuple-element.20, f32[384]{0:T(512)S(1)} %copy-done.6, f32[384]{0:T(512)S(1)} %copy-done.7, f32[128,64]{0,1:T(8,128)S(1)} %add_rsqrt_fusion.1, f32[128,64]{0,1:T(8,128)S(1)} %broadcast_multiply_fusion.1, bf16[2,384,1536]{2,1,0:T(8,128)(2,1)} %param.12, ...), kind=kOutput, calls=%fused_computation.74 | convolution fusion | flops 19468910592 | bytes 21302272 | tf_op jit(solution)/shard_map/btsf,fd->btsd/dot_general | solution.py:40
  349.2 6.5 %copy.17 = bf16[1,128,64,384]{3,2,0,1:T(8,128)(2,1)S(1)} copy(bf16[1,128,64,384]{3,1,2,0:T(8,128)(2,1)} %fusion.58) | data formatting | bytes 12582912 | tf_op jit(solution)/shard_map/convert_element_type | solution.py:41
  355.7 73.3 %all_to_all.27 = bf16[1,128,64,384]{3,2,0,1:T(8,128)(2,1)S(1)} all-to-all(bf16[1,128,64,384]{3,2,0,1:T(8,128)(2,1)S(1)} %copy.17), channel_id=1, replica_groups=mesh['data'=4,'sp'=4] {'sp'}, dimensions={1} | all-to-all | bytes 12582912 | tf_op jit(solution)/shard_map/all_to_all | solution.py:57
  428.9 3.5 copy.18
  (26 shorter events, 0.1 us)
Async XLA Ops:
  0.0 9.3 %copy-start.3 = (bf16[4,384]{1,0:T(4,128)(2,1)S(1)}, bf16[4,384]{1,0:T(4,128)(2,1)}, u32[]{:S(2)}) copy-start(bf16[4,384]{1,0:T(4,128)(2,1)} %param.8) | copy-start | bytes 9220
  0.0 9.3 %copy-start.2 = (bf16[4,384]{1,0:T(4,128)(2,1)S(1)}, bf16[4,384]{1,0:T(4,128)(2,1)}, u32[]{:S(2)}) copy-start(bf16[4,384]{1,0:T(4,128)(2,1)} %param.9) | copy-start | bytes 9220
  0.0 9.9 %copy-start.8 = (bf16[2,384,3,6,64]{1,4,3,2,0:T(8,128)(2,1)S(1)}, bf16[2,384,3,6,64]{1,4,3,2,0:T(8,128)(2,1)}, u32[]{:S(2)}) copy-start(bf16[2,384,3,6,64]{1,4,3,2,0:T(8,128)(2,1)} %param.10) | copy-start | bytes 5308420
  26.0 25.2 %copy-start.10 = (bf16[2,6,64,384]{3,2,1,0:T(8,128)(2,1)S(1)}, bf16[2,6,64,384]{3,2,1,0:T(8,128)(2,1)}, u32[]{:S(2)}) copy-start(bf16[2,6,64,384]{3,2,1,0:T(8,128)(2,1)} %param.11) | copy-start | bytes 1769476
  51.2 31.4 %copy-start = (bf16[2,1536,384]{2,1,0:T(8,128)(2,1)S(1)}, bf16[2,1536,384]{2,1,0:T(8,128)(2,1)}, u32[]{:S(2)}) copy-start(bf16[2,1536,384]{2,1,0:T(8,128)(2,1)} %param.13) | copy-start | bytes 7077892
  76.8 5.2 %copy-start.1 = (f32[32,256]{1,0:T(8,128)}, f32[32,256]{1,0:T(8,128)S(1)}, u32[]{:S(2)}) copy-start(f32[32,256]{1,0:T(8,128)S(1)} %broadcast_multiply_fusion.2) | copy-start | bytes 98308
  136.4 76.5 %all-to-all-start = ((bf16[1,32,256,384]{3,1,0,2:T(8,128)(2,1)}), bf16[1,32,256,384]{3,1,0,2:T(8,128)(2,1)}, u32[]{:S(2)}, u32[]{:S(2)}) async-start(bf16[1,32,256,384]{3,1,0,2:T(8,128)(2,1)} %copy.14), calls=%async_computation | async-start | bytes 12582912 | tf_op jit(solution)/shard_map/all_to_all | solution.py:55
  216.9 14.8 %copy-start.4 = (f32[384]{0:T(512)S(1)}, f32[384]{0:T(512)}, u32[]{:S(2)}) copy-start(f32[384]{0:T(512)} %get-tuple-element.12) | copy-start | bytes 4612
  216.9 14.8 %copy-start.5 = (f32[384]{0:T(512)S(1)}, f32[384]{0:T(512)}, u32[]{:S(2)}) copy-start(f32[384]{0:T(512)} %get-tuple-element.21) | copy-start | bytes 4612
  226.1 11.4 %copy-start.9 = (bf16[2,384,3,6,64]{1,4,3,2,0:T(8,128)(2,1)S(1)}, bf16[2,384,3,6,64]{1,4,3,2,0:T(8,128)(2,1)}, u32[]{:S(2)}) copy-start(bf16[2,384,3,6,64]{1,4,3,2,0:T(8,128)(2,1)} %param.10) | copy-start | bytes 5308420
  263.4 27.2 %copy-start.11 = (bf16[2,6,64,384]{3,2,1,0:T(8,128)(2,1)S(1)}, bf16[2,6,64,384]{3,2,1,0:T(8,128)(2,1)}, u32[]{:S(2)}) copy-start(bf16[2,6,64,384]{3,2,1,0:T(8,128)(2,1)} %param.11) | copy-start | bytes 1769476
  290.6 24.3 %copy-start.6 = (f32[384]{0:T(512)S(1)}, f32[384]{0:T(512)}, u32[]{:S(2)}) copy-start(f32[384]{0:T(512)} %get-tuple-element.9) | copy-start | bytes 4612
  290.6 24.3 %copy-start.7 = (f32[384]{0:T(512)S(1)}, f32[384]{0:T(512)}, u32[]{:S(2)}) copy-start(f32[384]{0:T(512)} %get-tuple-element.24) | copy-start | bytes 4612
where the time goes:
time: 441 us; the launch traced here: 433 us
  matrix products  190 us (43%)
  blocking collectives  73.3 us (17%)
  waiting for transfers between devices  71.2 us (16%)
  other arithmetic  63.6 us (14%)
  local copies, waits for them, and re-layouts  28.7 us (7%)
  starting transfers between devices  5.24 us (1%)
    dot_general x2, matrix products, finish_block(): jnp.einsum('btsf,fd->btsd', hidden, w_down_blk, preferred_element_type=jn...  78.6 us
    all_to_all x1, blocking collectives, local_run(): return lax.all_to_all(mixed_act, 'sp', 1, 2, tiled=True)  73.3 us
    all_to_all x1, waiting for transfers between devices, local_run(): mixed_act = lax.all_to_all(mixed_act, 'sp', 2, 1, tiled=True)  71.2 us
    dot_general x2, matrix products, finish_block(): jnp.einsum('btshk,hkd->btsd', attended, w_out_blk, preferred_element_type...  44.5 us
    dot_general x2, matrix products, project_qkv(): jnp.einsum('btsd,dchk->btschk', normed, w_qkv_blk, preferred_element_type...  29 us
    sub x1, other arithmetic, attend(): attn_probs = jax.nn.softmax(scores, axis=-1).astype(jnp.bfloat16)  27.2 us
    sub x1, matrix products, attend(): attn_probs = jax.nn.softmax(scores, axis=-1).astype(jnp.bfloat16)  25.2 us
    reduce_sum x4, other arithmetic, layer_norm(): variance = jnp.mean(centered * centered, axis=-1, keepdims=True)  21.2 us
  transfers between devices with their start and end apart: 1, of which 1 were waited for; matrix products, arithmetic and copies ran while one was open for 0% of the time, Pallas kernels for 0%

commit v1 on v0

v1 whole, which is shorter than its diff:
```python
import functools

import jax
import jax.numpy as jnp
from jax import lax
from jax.experimental import pallas as pl
from jax.experimental.pallas import tpu as pltpu
from jax.sharding import PartitionSpec as P

BF, F32 = jnp.bfloat16, jnp.float32
D, H, DH, F = 384, 6, 64, 1536
T = 256
EPS = 1e-6
C_EXP = 0.125 * 1.4426950408889634
G0, G1 = 0.7978845608028654, 0.044715
RB = 64
NSLOT = 4
MESH_ID = pl.DeviceIdType.MESH


def dot(a, b):
    return jnp.dot(a, b, preferred_element_type=F32)


def psum(v):
    return jnp.sum(v.reshape(v.shape[0] // 8, 8, v.shape[1]), axis=0)


def dup(r):
    return jnp.concatenate([r, r], axis=1)


def full_mean(acc):
    return jnp.sum(acc, axis=0, keepdims=True) * (1.0 / D)


def gelu_of_half(z):
    return (z + z * jnp.tanh(z * (z * z * (8 * G0 * G1) + 2 * G0))).astype(BF)


def ln_p1(xn, x_ring, xf_s):
    x_ring[...] = xn
    acc = None
    for r in range(0, D, RB):
        f = xn[r:r + RB].astype(F32)
        xf_s[pl.ds(r, RB), :] = f
        t = psum(f)
        acc = t if acc is None else acc + t
    return full_mean(acc)


def ln2_p1(x_ring, pr, hf_s):
    acc = None
    for r in range(0, D, RB):
        f = (x_ring[pl.ds(r, RB), :].astype(F32) + pr[r:r + RB]).astype(BF).astype(F32)
        hf_s[pl.ds(r, RB), :] = f
        t = psum(f)
        acc = t if acc is None else acc + t
    return full_mean(acc)


def ln_p2(f_s, mean):
    acc = None
    for r in range(0, D, RB):
        c = f_s[pl.ds(r, RB), :] - mean
        t = psum(c * c)
        acc = t if acc is None else acc + t
    return lax.rsqrt(full_mean(acc) + EPS)


def ln_p3(f_s, mean, rstd, g_ref, b_ref, out):
    for r in range(0, D, RB):
        c = f_s[pl.ds(r, RB), :] - mean
        out[pl.ds(r, RB), :] = (c * rstd * dup(g_ref[pl.ds(r, RB), :]) + dup(b_ref[pl.ds(r, RB), :])).astype(BF)


def softmax_half(s):
    m = jnp.max(s, axis=0, keepdims=True)
    e = jnp.exp2((s - m) * C_EXP)
    return e.astype(BF), jnp.sum(e, axis=0, keepdims=True)


def setup_weights(gain_ref, bias_ref, wout_ref, wup_ref, wdown_ref, wo_s, wu_s, wd_s, gb_s, layer):
    wo_s[...] = wout_ref[0].T
    wu_s[...] = wup_ref[0].T * 0.5
    wd_s[...] = wdown_ref[0].T
    for i, r in enumerate((gain_ref, bias_ref)):
        for j in range(2):
            row = r[pl.ds(2 * layer + j, 1), :].astype(F32)
            gb_s[2 * i + j] = jnp.broadcast_to(row, (128, D)).T


def block_step(i, layer, xn, wqkv, wo_s, wu_s, wd_s, gb_s, x_s, a_s, qkv_s, o_s, u_s, a2_s, xf_s, hf_s):
    cur = jnp.bitwise_and(i, 1)
    nxt = 1 - cur
    zs, ss, es, os = {}, {}, {}, {}
    qc, qn = qkv_s.at[cur], qkv_s.at[nxt]
    an, a_out = a_s.at[nxt], a_s.at[cur]
    op, on = o_s.at[nxt], o_s.at[cur]

    def up(j):
        zs[j] = [dot(wu_s[pl.ds(256 * j + 128 * t, 128), :], a2_s[...]) for t in range(2)]

    def act(j):
        for t, z in enumerate(zs.pop(j)):
            u_s[pl.ds(256 * j + 128 * t, 128), :] = gelu_of_half(z)

    def lanes(h):
        return pl.ds(128 * (h // 3), 128)

    def S(h):
        if layer == 0:
            ss[h] = dot(qc[pl.ds(D + h * DH, DH), :].T, qc[pl.ds(h * DH, DH), :])
        else:
            c, r = lanes(h), 128 * (h % 3)
            q0, q1 = qc[pl.ds(r, 64), c], qc[pl.ds(r + 64, 64), c]
            z = jnp.zeros_like(q0)
            q = jnp.concatenate([jnp.concatenate([q0, z], axis=1), jnp.concatenate([z, q1], axis=1)], axis=0)
            ss[h] = dot(qc[pl.ds(D + r, 128), c].T, q)

    def Pm(h):
        s = ss.pop(h)
        e0, l0 = softmax_half(s[:, :128])
        e1, l1 = softmax_half(s[:, 128:])
        es[h] = (jnp.concatenate([e0, e1], axis=1), jnp.concatenate([l0, l1], axis=1))

    def PV(h):
        if layer == 0:
            os[h] = dot(qc[pl.ds(2 * D + h * DH, DH), :], es[h][0])
        else:
            os[h] = dot(qc[pl.ds(2 * D + 128 * (h % 3), 128), lanes(h)], es[h][0])

    def OS(h):
        o, r = os.pop(h), 1.0 / es.pop(h)[1]
        if layer == 0:
            on[pl.ds(h * DH, DH), :] = (o * r).astype(BF)
        else:
            k, c = 128 * (h % 3), lanes(h)
            on[pl.ds(k, 64), c] = (o[:64, :128] * r[:, :128]).astype(BF)
            on[pl.ds(k + 64, 64), c] = (o[64:, 128:] * r[:, 128:]).astype(BF)

    def Q(c):
        for t in range(2):
            qn[pl.ds(c * D + 192 * t, 192), :] = dot(wqkv[0, pl.ds(c * D + 192 * t, 192), :], an[...]).astype(BF)

    def dn(k):
        return [dot(wd_s[pl.ds(192 * t, 192), 256 * k:256 * k + 256], u_s[pl.ds(256 * k, 256), :]) for t in range(2)]

    def addl(*parts):
        return [functools.reduce(lambda a, b: a + b, z) for z in zip(*parts)]

    pr = jnp.concatenate([dot(wo_s[pl.ds(192 * t, 192), :], op[...]) for t in range(2)], axis=0)
    S(0)
    Q(0)
    mean2 = ln2_p1(x_s.at[jnp.bitwise_and(i + 3, 3)], pr, hf_s)
    S(1); Pm(0)
    rstd2 = ln_p2(hf_s, mean2)
    Q(1)
    ln_p3(hf_s, mean2, rstd2, gb_s.at[1], gb_s.at[3], a2_s)
    PV(0)
    up(0)
    Pm(1)
    Q(2)
    S(2)
    up(1); act(0)
    OS(0); PV(1)
    up(2); act(1)
    Pm(2); S(3); up(3)
    PV(2); OS(1); act(2)
    Pm(3); S(4); up(4)
    PV(3); OS(2); act(3)
    Pm(4); S(5); up(5)
    PV(4); OS(3); act(4)
    Pm(5)
    yd = addl(dn(0), dn(1))
    PV(5); OS(4); act(5)
    yd = addl(yd, dn(2), dn(3))
    mean1 = ln_p1(xn(), x_s.at[jnp.bitwise_and(i + 2, 3)], xf_s)
    OS(5)
    rstd1 = ln_p2(xf_s, mean1)
    yd = addl(yd, dn(4), dn(5))
    ln_p3(xf_s, mean1, rstd1, gb_s.at[0], gb_s.at[2], a_out)
    y = hf_s[...] + jnp.concatenate(yd, axis=0)
    return y.T.astype(BF)


def prologue(xns, wqkv, gb_s, x_s, a_s, qkv_s, o_s, xf_s):
    for t in range(2):
        mean = ln_p1(xns[t](), x_s.at[t], xf_s)
        ln_p3(xf_s, mean, ln_p2(xf_s, mean), gb_s.at[0], gb_s.at[2], a_s.at[t])
    qkv_s[0] = dot(wqkv[0], a_s[0]).astype(BF)
    o_s[...] = jnp.zeros_like(o_s)
    x_s[3] = jnp.zeros((D, T), BF)


def greet(axis, n):
    me = lax.axis_index(axis)
    barrier = pltpu.get_barrier_semaphore()
    for k in range(1, n):
        pl.semaphore_signal(barrier, inc=1, device_id={axis: lax.rem(me + k, n)}, device_id_type=MESH_ID)
    pl.semaphore_wait(barrier, n - 1)


def exchange(axis, n, src, dst, local_sem, send_sem, recv_sem):
    me = lax.axis_index(axis)
    out = [pltpu.make_async_copy(src(me), dst, local_sem)]
    for k in range(1, n):
        to = lax.rem(me + k, n)
        out.append(pltpu.make_async_remote_copy(
            src_ref=src(to), dst_ref=dst, send_sem=send_sem.at[k - 1], recv_sem=recv_sem.at[k - 1],
            device_id={axis: to}, device_id_type=MESH_ID))
    return out


def send_step(i, steps, axis, n, y, ybuf, tile_copies, local_sem, send_sem, recv_sem, recv_part):
    f = i - 1
    slot = lax.rem(i + NSLOT - 1, NSLOT)

    @pl.when(f >= NSLOT)
    def _():
        cs = tile_copies(f - NSLOT, slot)
        cs[0].wait()
        for c in cs[1:]:
            c.wait_send()

    y()

    @pl.when(f >= 0)
    def _():
        for c in tile_copies(f, slot):
            c.start()

    @pl.when(f == steps - 1)
    def _():
        for b in range(NSLOT):
            g = steps - NSLOT + b
            cs = tile_copies(g, g % NSLOT)
            cs[0].wait()
            for c in cs[1:]:
                c.wait_send()
        for k in range(n - 1):
            pltpu.make_async_copy(recv_part, recv_part, recv_sem.at[k]).wait()


def space_kernel(axis, n, steps, xn_ref, gain_ref, bias_ref, wqkv, wout_ref, wup_ref, wdown_ref, x0_ref, z_ref,
                 wo_s, wu_s, wd_s, gb_s, x_s, a_s, qkv_s, o_s, u_s, a2_s, xf_s, hf_s, ybuf, local_sem, send_sem, recv_sem):
    i = pl.program_id(0)
    me = lax.axis_index(axis)
    part = T // n

    @pl.when(i == 0)
    def _():
        greet(axis, n)
        setup_weights(gain_ref, bias_ref, wout_ref, wup_ref, wdown_ref, wo_s, wu_s, wd_s, gb_s, 0)
        prologue([lambda: x0_ref[0].T, lambda: x0_ref[1].T], wqkv, gb_s, x_s, a_s, qkv_s, o_s, xf_s)

    def tile_copies(f, slot):
        return exchange(axis, n, lambda k: ybuf.at[slot, pl.ds(pl.multiple_of(part * k, part), part)],
                        z_ref.at[me * steps + f], local_sem.at[slot], send_sem.at[slot], recv_sem)

    def y():
        ybuf[lax.rem(i + NSLOT - 1, NSLOT)] = block_step(
            i, 0, lambda: xn_ref[0].T, wqkv, wo_s, wu_s, wd_s, gb_s, x_s, a_s, qkv_s, o_s, u_s, a2_s, xf_s, hf_s)

    send_step(i, steps, axis, n, y, ybuf, tile_copies, local_sem, send_sem, recv_sem, z_ref.at[pl.ds(0, steps)])


def time_kernel(axis, n, steps, zn_ref, gain_ref, bias_ref, wqkv, wout_ref, wup_ref, wdown_ref, z0_ref, w_ref,
                wo_s, wu_s, wd_s, gb_s, x_s, a_s, qkv_s, o_s, u_s, a2_s, xf_s, hf_s, ybuf, local_sem, send_sem, recv_sem, c_s):
    i = pl.program_id(0)
    me = lax.axis_index(axis)
    part = 128 // n

    def convert(z, chunk, q):
        v = z.astype(F32).reshape(256, D)
        for j in range(3):
            c_s[chunk, j, pl.ds(pl.multiple_of(256 * q, 256), 256), :] = v[:, 128 * j:128 * j + 128]

    def tile(chunk, pair):
        return jnp.concatenate([
            jnp.concatenate([c_s[chunk, j, pl.ds(2 * pair + t, 128, stride=8), :].astype(BF).T for t in range(2)], axis=1)
            for j in range(3)], axis=0)

    @pl.when(i == 0)
    def _():
        greet(axis, n)
        setup_weights(gain_ref, bias_ref, wout_ref, wup_ref, wdown_ref, wo_s, wu_s, wd_s, gb_s, 1)
        for q in range(4):
            convert(z0_ref[pl.ds(32 * q, 32), pl.ds(0, 8), :], 0, q)
        for q in range(2):
            convert(z0_ref[pl.ds(32 * q, 32), pl.ds(8, 8), :], 1, q)
        prologue([lambda: tile(0, 0), lambda: tile(0, 1)], wqkv, gb_s, x_s, a_s, qkv_s, o_s, xf_s)

    def tile_copies(f, slot):
        return exchange(axis, n, lambda k: ybuf.at[slot, :, pl.ds(pl.multiple_of(part * k, part), part)],
                        w_ref.at[pl.ds(2 * (me * steps + f), 2)], local_sem.at[slot], send_sem.at[slot], recv_sem)

    def y():
        t = i + 2
        q = jnp.bitwise_and(t, 3)
        chunk = jnp.bitwise_and(lax.shift_right_logical(t, 2), 1)
        out = block_step(
            i, 1, lambda: tile(chunk, q), wqkv, wo_s, wu_s, wd_s, gb_s, x_s, a_s, qkv_s, o_s, u_s, a2_s, xf_s, hf_s)
        ybuf[lax.rem(i + NSLOT - 1, NSLOT)] = out.reshape(2, 128, D)
        convert(zn_ref[pl.ds(pl.multiple_of(32 * q, 32), 32)], 1 - chunk, q)

    send_step(i, steps, axis, n, y, ybuf, tile_copies, local_sem, send_sem, recv_sem, w_ref.at[pl.ds(0, 2 * steps)])


def swap_kernel(w_ref, out_ref, s_ref):
    k = w_ref.shape[0]
    v = w_ref[...].astype(F32).reshape(k * 32, D)
    for j in range(3):
        s_ref[j] = v[:, 128 * j:128 * j + 128]
    for f in range(32):
        for j in range(3):
            out_ref[f, :, 128 * j:128 * j + 128] = s_ref[j, pl.ds(f, k, stride=32), :].astype(BF)


def weight_spec(shape, layer):
    return pl.BlockSpec((1,) + shape, lambda i: (layer, 0, 0), pipeline_mode=pl.Buffered(1))


def solution(mesh):
    axis = 'sp'
    n = mesh.shape[axis]
    steps = 32
    act_spec = P('data', axis, None, None)

    def block(kernel, layer, x, xspec, x0spec, out_shape, ybuf, weights, extra):
        small = pl.BlockSpec((4, D), lambda i: (0, 0), pipeline_mode=pl.Buffered(1))
        flops = 2 * steps * T * (3 * D * D + D * D + 2 * D * F + 2 * D * T)
        return pl.pallas_call(
            functools.partial(kernel, axis, n, steps),
            grid=(steps + 1,),
            out_shape=out_shape,
            in_specs=[xspec, small, small, weight_spec((3 * D, D), layer), weight_spec((D, D), layer),
                      weight_spec((D, F), layer), weight_spec((F, D), layer), x0spec],
            out_specs=pl.BlockSpec(memory_space=pl.ANY),
            scratch_shapes=[
                pltpu.VMEM((D, D), BF), pltpu.VMEM((F, D), BF), pltpu.VMEM((D, F), BF),
                pltpu.VMEM((4, D, 128), F32),
                pltpu.VMEM((4, D, T), BF), pltpu.VMEM((2, D, T), BF),
                pltpu.VMEM((2, 3 * D, T), BF), pltpu.VMEM((2, D, T), BF), pltpu.VMEM((F, T), BF),
                pltpu.VMEM((D, T), BF),
                pltpu.VMEM((D, T), F32), pltpu.VMEM((D, T), F32),
                ybuf,
                pltpu.SemaphoreType.DMA((NSLOT,)), pltpu.SemaphoreType.DMA((NSLOT, n - 1)), pltpu.SemaphoreType.DMA((n - 1,)),
            ] + extra,
            compiler_params=pltpu.CompilerParams(
                dimension_semantics=("arbitrary",), vmem_limit_bytes=60 << 20,
                collective_id=layer, has_side_effects=True),
            cost_estimate=pl.CostEstimate(flops=flops, bytes_accessed=4 * steps * T * D, transcendentals=0),
            name=('space_block', 'time_block')[layer],
        )(x, *weights, x)

    def local_run(latent, ln_gain, ln_bias, w_qkv, w_out, w_up, w_down):
        weights = (ln_gain, ln_bias, jnp.transpose(w_qkv, (0, 2, 3, 4, 1)).reshape(2, 3 * D, D), w_out.reshape(2, D, D), w_up, w_down)
        x = latent[0]
        z = block(
            space_kernel, 0, x,
            pl.BlockSpec((1, T, D), lambda i: (jnp.minimum(i + 2, steps - 1), 0, 0)),
            pl.BlockSpec((2, T, D), lambda i: (0, 0, 0), pipeline_mode=pl.Buffered(1)),
            jax.ShapeDtypeStruct((128, 64, D), BF), pltpu.VMEM((NSLOT, T, D), BF), weights, [])
        w = block(
            time_kernel, 1, z,
            pl.BlockSpec((128, 8, D), lambda i: (0, jnp.minimum((i + 6) // 4, 7), 0)),
            pl.BlockSpec((128, 16, D), lambda i: (0, 0, 0), pipeline_mode=pl.Buffered(1)),
            jax.ShapeDtypeStruct((256, 32, D), BF), pltpu.VMEM((NSLOT, 2, 128, D), BF), weights,
            [pltpu.VMEM((2, 3, 1024, 128), F32)])
        out = pl.pallas_call(
            swap_kernel,
            grid=(16,),
            out_shape=jax.ShapeDtypeStruct((32, 256, D), BF),
            in_specs=[pl.BlockSpec((16, 32, D), lambda i: (i, 0, 0))],
            out_specs=pl.BlockSpec((32, 16, D), lambda i: (0, i, 0)),
            scratch_shapes=[pltpu.VMEM((3, 16 * 32, 128), F32)],
            name='swap',
        )(w)
        return out[None]

    return jax.shard_map(local_run, mesh=mesh, in_specs=(act_spec, P(), P(), P(), P(), P(), P()), out_specs=act_spec, check_vma=False)
```

time: 441 us -> 173 us (0.39); the launches traced: 433 us -> 172 us
  matrix products: 190 us -> 0 us
  Pallas kernels: 0 us -> 172 us
  blocking collectives: 73.3 us -> 0 us
  waiting for transfers between devices: 71.2 us -> 0 us
  other arithmetic: 63.6 us -> 0 us
  local copies, waits for them, and re-layouts: 28.7 us -> 0 us
  starting transfers between devices: 5.24 us -> 0 us
    pallas_call x0 -> x3, Pallas kernels: none -> 172 us  [the longest x2 158 us: block(): pl.pallas_call(functools.partial(kernel, axis, n, steps), grid=(steps + 1...]
    dot_general x7 -> x0, matrix products: 165 us -> none  [the longest x2 78.6 us: finish_block(): jnp.einsum('btsf,fd->btsd', hidden, w_down_blk, preferred_element_type=jn...]
    all_to_all x1 -> x0, blocking collectives: 73.3 us -> none  [local_run(): return lax.all_to_all(mixed_act, 'sp', 1, 2, tiled=True)]
    all_to_all x1 -> x0, waiting for transfers between devices: 71.2 us -> none  [local_run(): mixed_act = lax.all_to_all(mixed_act, 'sp', 2, 1, tiled=True)]
    reduce_sum x6 -> x0, other arithmetic: 29.2 us -> none  [the longest x4 21.2 us: layer_norm(): variance = jnp.mean(centered * centered, axis=-1, keepdims=True)]
    sub x1 -> x0, other arithmetic: 27.2 us -> none  [attend(): attn_probs = jax.nn.softmax(scores, axis=-1).astype(jnp.bfloat16)]
    sub x1 -> x0, matrix products: 25.2 us -> none  [attend(): attn_probs = jax.nn.softmax(scores, axis=-1).astype(jnp.bfloat16)]
    convert_element_type x3 -> x0, local copies, waits for them, and re-layouts: 24.9 us -> none  [the longest x2 15.7 us: finish_block(): return result.astype(jnp.bfloat16)]
  transfers between devices with their start and end apart: 1 -> 0, of which waited for: 1 -> 0; matrix products, arithmetic and copies ran while one was open for 0% -> 0% of each run, Pallas kernels for 0% -> 0%
where the time goes in v1:
time: 173 us; the launch traced here: 172 us
  Pallas kernels  172 us (99%)
    pallas_call x2, Pallas kernels, block(): pl.pallas_call(functools.partial(kernel, axis, n, steps), grid=(steps + 1...  158 us
    pallas_call x1, Pallas kernels, local_run(): pl.pallas_call(swap_kernel, grid=(16,), out_shape=jax.ShapeDtypeStruct((3...  14.7 us

profile of v1, /device:TPU:0, one launch (start us, length us, event | category | flops | bytes accessed | tf_op | source)
XLA Modules:
  0.0 172.5 jit_solution(4351470866761162682)
XLA Ops:
  0.0 79.4 %space_block.1.zn_ref.z0_ref = bf16[128,64,384]{2,1,0:T(8,128)(2,1)} custom-call(bf16[32,256,384]{2,1,0:T(8,128)(2,1)} %bitcast.6, bf16[4,384]{1,0:T(4,128)(2,1)} %gain_ref.3, bf16[4,384]{1,0:T(4,128)(2,1)} %bias_ref.3, bf16[2,1152,384]{2,1,0:T(8,128)(2,1)} %bitcast.8, bf16[2,384,384]{2,1,0:T(8,128)(2,1)} %bitcast.10, bf16[2,384,1536]{2,1,0:T(8,128)(2,1)} %wup_ref.3, ...), custom_call_target="tpu_custom_call" | custom-call | flops 32212254720 | bytes 12582912 | tf_op jit(solution)/shard_map/space_block/pallas_call | solution.py:333
  79.4 78.3 %time_block.1.w_ref = bf16[256,32,384]{2,1,0:T(8,128)(2,1)} custom-call(bf16[128,64,384]{2,1,0:T(8,128)(2,1)} %space_block.1.zn_ref.z0_ref, bf16[4,384]{1,0:T(4,128)(2,1)} %gain_ref.3, bf16[4,384]{1,0:T(4,128)(2,1)} %bias_ref.3, bf16[2,1152,384]{2,1,0:T(8,128)(2,1)} %bitcast.9, bf16[2,384,384]{2,1,0:T(8,128)(2,1)} %bitcast.11, ...), custom_call_target="tpu_custom_call" | custom-call | flops 32212254720 | bytes 12582912 | tf_op jit(solution)/shard_map/time_block/pallas_call | solution.py:333
  157.8 14.7 %swap.1 = bf16[32,256,384]{2,1,0:T(8,128)(2,1)} custom-call(bf16[256,32,384]{2,1,0:T(8,128)(2,1)} %time_block.1.w_ref), custom_call_target="tpu_custom_call" | custom-call | tf_op jit(solution)/shard_map/swap/pallas_call | solution.py:371
